TPU v7x, 32 devices: a whole 2x2x4 slice. The times are simulated.
32 devices in a mesh: dp: 8 (over y, x, core), tensor: 4 (over z).
Axes of the slice: x: 2, y: 2, z: 4, core: 2. Of those that a mesh axis runs over, the one named last changes fastest.
Arguments:
- tokens: bfloat16 [8192, 2048], P('dp'), may hold values from -6 to 6
- attn_norm_gain: float32 [2048], replicated, may hold values from 0.5 to 1.5
- attn_norm_bias: float32 [2048], replicated, may hold values from -1.8 to 1.8
- mlp_norm_gain: float32 [2048], replicated, may hold values from 0.5 to 1.5
- mlp_norm_bias: float32 [2048], replicated, may hold values from -1.8 to 1.8
- w_qkv: bfloat16 [2048, 6144], P(None, 'tensor'), may hold values from -0.125 to 0.125
- qkv_bias: float32 [6144], P('tensor'), may hold values from -3 to 3
- w_out: bfloat16 [2048, 2048], P('tensor'), may hold values from -0.75 to 0.75
- w_up: bfloat16 [2048, 8192], P(None, 'tensor'), may hold values from -0.125 to 0.125
- up_bias: float32 [8192], P('tensor'), may hold values from -3 to 3
- w_down: bfloat16 [8192, 2048], P('tensor'), may hold values from -0.0625 to 0.0625
- out_bias: float32 [2048], replicated, may hold values from -3 to 3
- cotangent: bfloat16 [8192, 2048], P('dp'), may hold values from -6 to 6
Outputs:
- block_out: bfloat16 [8192, 2048], P('dp')
- input_grad: float32 [8192, 2048], P('dp')
- grad_w_qkv: float32 [2048, 6144], P('dp', 'tensor')
- grad_w_out: float32 [2048, 2048], P('tensor', 'dp')
- grad_w_up: float32 [2048, 8192], P('dp', 'tensor')
- grad_w_down: float32 [8192, 2048], P('tensor', 'dp')
- grad_norm_params: float32 [4, 2048], replicated
- grad_qkv_bias: float32 [6144], replicated
- grad_up_bias: float32 [8192], replicated
- grad_out_bias: float32 [2048], replicated
All inputs are finite; a program needn't handle non-finite values.
Results may differ from a plain program's by a relative error of at most 0.012.
Values may be sent and summed in bfloat16 or wider, within the bound.
A program may use at most 192 MiB of HBM per device.

v0:
```python
import jax
import jax.numpy as jnp
from jax import lax
from jax.sharding import PartitionSpec as P

H = 8
HD = 256
FF = 8192
ROT = 64
SEQ_LEN = 1024
EPSILON = 1e-05
ROPE_BASE = 10000.0
MASKED = -1e30


def layer_stats(tokens_f):
    row_mean = jnp.mean(tokens_f, axis=1, keepdims=True)
    centred = tokens_f - row_mean
    variance = jnp.mean(centred * centred, axis=1, keepdims=True)
    inv_std = lax.rsqrt(variance + EPSILON)
    return (centred * inv_std, inv_std)


def rotary_tables(length):
    half_rot = ROT // 2
    freqs = ROPE_BASE ** (-(2.0 * jnp.arange(half_rot, dtype=jnp.float32)) / ROT)
    angles = jnp.arange(length, dtype=jnp.float32)[:, None] * freqs[None, :]
    return (jnp.cos(angles), jnp.sin(angles))


def rotate(values, cosine_table, sine_table):
    half_rot = ROT // 2
    first_half = values[..., :half_rot]
    second_half = values[..., half_rot:ROT]
    cos_rows = cosine_table[:, None, :]
    sin_rows = sine_table[:, None, :]
    return jnp.concatenate(
        [
            first_half * cos_rows - second_half * sin_rows,
            second_half * cos_rows + first_half * sin_rows,
            values[..., ROT:],
        ],
        axis=-1,
    )


def unrotate(grads, cosine_table, sine_table):
    half_rot = ROT // 2
    first_half = grads[..., :half_rot]
    second_half = grads[..., half_rot:ROT]
    cos_rows = cosine_table[:, None, :]
    sin_rows = sine_table[:, None, :]
    return jnp.concatenate(
        [
            first_half * cos_rows + second_half * sin_rows,
            second_half * cos_rows - first_half * sin_rows,
            grads[..., ROT:],
        ],
        axis=-1,
    )


def masked_scores(query_block, keys_all, block_start):
    scaling = float(HD) ** (-0.5)
    scores = (
        jnp.einsum("sqhd,skhd->shqk", query_block, keys_all, preferred_element_type=jnp.float32)
        * scaling
    )
    query_pos = block_start + jnp.arange(query_block.shape[1])
    key_pos = jnp.arange(keys_all.shape[1])
    causal = key_pos[None, :] <= query_pos[:, None]
    return jnp.where(causal[None, None], scores, MASKED)


def attention_forward(queries, keys_all, values_all):
    length = queries.shape[1]
    block_rows = min(512, length)
    outputs = []
    log_parts = []
    for block_start in range(0, length, block_rows):
        query_block = queries[:, block_start : block_start + block_rows]
        scores = masked_scores(query_block, keys_all, block_start)
        row_top = jnp.max(scores, axis=-1, keepdims=True)
        log_total = row_top + jnp.log(jnp.sum(jnp.exp(scores - row_top), axis=-1, keepdims=True))
        soft_probs = jnp.exp(scores - log_total).astype(jnp.bfloat16)
        outputs.append(
            jnp.einsum(
                "shqk,skhd->sqhd", soft_probs, values_all, preferred_element_type=jnp.float32
            )
        )
        log_parts.append(log_total)
    return (jnp.concatenate(outputs, axis=1), jnp.concatenate(log_parts, axis=2))


def attention_backward(queries, keys_all, values_all, log_sums, grad_blocks):
    length = queries.shape[1]
    block_rows = min(512, length)
    scaling = float(HD) ** (-0.5)
    query_grads = []
    key_grad = jnp.zeros(keys_all.shape, jnp.float32)
    value_grad = jnp.zeros(values_all.shape, jnp.float32)
    for block_start in range(0, length, block_rows):
        query_block = queries[:, block_start : block_start + block_rows]
        grad_block = grad_blocks[:, block_start : block_start + block_rows]
        scores = masked_scores(query_block, keys_all, block_start)
        soft_probs = jnp.exp(scores - log_sums[:, :, block_start : block_start + block_rows])
        prob_grad = jnp.einsum(
            "sqhd,skhd->shqk", grad_block, values_all, preferred_element_type=jnp.float32
        )
        value_grad = value_grad + jnp.einsum(
            "shqk,sqhd->skhd",
            soft_probs.astype(jnp.bfloat16),
            grad_block,
            preferred_element_type=jnp.float32,
        )
        row_dot = jnp.sum(soft_probs * prob_grad, axis=-1, keepdims=True)
        score_grad = (soft_probs * (prob_grad - row_dot)).astype(jnp.bfloat16)
        query_grads.append(
            jnp.einsum("shqk,skhd->sqhd", score_grad, keys_all, preferred_element_type=jnp.float32)
            * scaling
        )
        key_grad = (
            key_grad
            + jnp.einsum(
                "shqk,sqhd->skhd", score_grad, query_block, preferred_element_type=jnp.float32
            )
            * scaling
        )
    return (jnp.concatenate(query_grads, axis=1), key_grad, value_grad)


def norm_back(seed_rows, scale_rows, normed_rows, grad_rows):
    grad_mean = jnp.mean(grad_rows, axis=1, keepdims=True)
    cross_mean = jnp.mean(grad_rows * normed_rows, axis=1, keepdims=True)
    return seed_rows.astype(jnp.float32) + scale_rows * (
        grad_rows - grad_mean - normed_rows * cross_mean
    )


def per_device(
    tokens,
    attn_norm_gain,
    attn_norm_bias,
    mlp_norm_gain,
    mlp_norm_bias,
    w_qkv,
    qkv_bias,
    w_out,
    w_up,
    up_bias,
    w_down,
    out_bias,
    cotangent,
):
    row_count = tokens.shape[0]
    seq_count = row_count // SEQ_LEN
    local_heads = w_qkv.shape[1] // (3 * HD)
    tokens_f = tokens.astype(jnp.float32)
    normed, inv_std = layer_stats(tokens_f)
    attn_in = (normed * attn_norm_gain + attn_norm_bias).astype(jnp.bfloat16)
    mlp_in = (normed * mlp_norm_gain + mlp_norm_bias).astype(jnp.bfloat16)
    projected = jnp.dot(attn_in, w_qkv, preferred_element_type=jnp.float32) + qkv_bias
    projected = projected.reshape(seq_count, SEQ_LEN, local_heads, 3, HD)
    cosine_table, sine_table = rotary_tables(SEQ_LEN)
    queries = rotate(projected[:, :, :, 0], cosine_table, sine_table).astype(jnp.bfloat16)
    keys_all = rotate(projected[:, :, :, 1], cosine_table, sine_table).astype(jnp.bfloat16)
    values_all = projected[:, :, :, 2].astype(jnp.bfloat16)
    attended, log_sums = attention_forward(queries, keys_all, values_all)
    attended = attended.astype(jnp.bfloat16).reshape(row_count, local_heads * HD)
    up_pre = jnp.dot(mlp_in, w_up, preferred_element_type=jnp.float32) + up_bias
    hidden = jax.nn.gelu(up_pre, approximate=False).astype(jnp.bfloat16)
    branch_terms = jnp.dot(attended, w_out, preferred_element_type=jnp.float32) + jnp.dot(
        hidden, w_down, preferred_element_type=jnp.float32
    )
    share_rows = row_count // lax.axis_size("tensor")
    row_start = lax.axis_index("tensor") * share_rows
    branch_total = lax.psum(branch_terms, "tensor")
    block_out = (tokens_f + branch_total + out_bias).astype(jnp.bfloat16)
    hidden_grad = jnp.einsum("td,fd->tf", cotangent, w_down, preferred_element_type=jnp.float32)
    gelu_pull = jax.vjp(lambda pre_act: jax.nn.gelu(pre_act, approximate=False), up_pre)[1]
    up_grad = gelu_pull(hidden_grad)[0].astype(jnp.bfloat16)
    grad_down_local = jnp.einsum("tf,td->fd", hidden, cotangent, preferred_element_type=jnp.float32)
    grad_up_local = jnp.einsum("tc,tf->cf", mlp_in, up_grad, preferred_element_type=jnp.float32)
    mlp_in_grad = jnp.einsum("tf,cf->tc", up_grad, w_up, preferred_element_type=jnp.float32)
    up_bias_grad = jnp.sum(up_grad, axis=0, dtype=jnp.float32)
    attended_grad = jnp.einsum("td,ed->te", cotangent, w_out, preferred_element_type=jnp.float32)
    attended_grad = attended_grad.astype(jnp.bfloat16)
    grad_out_local = jnp.einsum(
        "te,td->ed", attended, cotangent, preferred_element_type=jnp.float32
    )
    grad_blocks = attended_grad.reshape(seq_count, SEQ_LEN, local_heads, HD)
    query_grad, key_grad, value_grad = attention_backward(
        queries, keys_all, values_all, log_sums, grad_blocks
    )
    projected_grad = jnp.stack(
        [
            unrotate(query_grad, cosine_table, sine_table),
            unrotate(key_grad, cosine_table, sine_table),
            value_grad,
        ],
        axis=3,
    )
    projected_grad = projected_grad.reshape(row_count, local_heads * 3 * HD).astype(jnp.bfloat16)
    grad_qkv_local = jnp.einsum(
        "tc,te->ce", attn_in, projected_grad, preferred_element_type=jnp.float32
    )
    qkv_bias_grad = jnp.sum(projected_grad, axis=0, dtype=jnp.float32)
    attn_in_grad = jnp.einsum(
        "te,ce->tc", projected_grad, w_qkv, preferred_element_type=jnp.float32
    )
    grad_w_qkv, grad_w_out, grad_w_up, grad_w_down = (
        lax.psum_scatter(grad_qkv_local, "dp", scatter_dimension=0, tiled=True),
        lax.psum_scatter(grad_out_local, "dp", scatter_dimension=1, tiled=True),
        lax.psum_scatter(grad_up_local, "dp", scatter_dimension=0, tiled=True),
        lax.psum_scatter(grad_down_local, "dp", scatter_dimension=1, tiled=True),
    )
    norm_terms = jnp.stack(
        [
            jnp.sum(attn_in_grad * normed, axis=0),
            jnp.sum(attn_in_grad, axis=0),
            jnp.sum(mlp_in_grad * normed, axis=0),
            jnp.sum(mlp_in_grad, axis=0),
        ]
    )
    normed_part = attn_in_grad * attn_norm_gain + mlp_in_grad * mlp_norm_gain
    normed_grad = lax.psum(normed_part, "tensor")
    input_grad = norm_back(cotangent, inv_std, normed, normed_grad)
    tensor_index = lax.axis_index("tensor")
    qkv_full = lax.dynamic_update_slice(
        jnp.zeros((3 * H * HD,), jnp.float32),
        qkv_bias_grad,
        (tensor_index * qkv_bias_grad.shape[0],),
    )
    up_full = lax.dynamic_update_slice(
        jnp.zeros((FF,), jnp.float32), up_bias_grad, (tensor_index * up_bias_grad.shape[0],)
    )
    out_bias_part = jnp.sum(
        lax.dynamic_slice_in_dim(cotangent, row_start, share_rows, 0), axis=0, dtype=jnp.float32
    )
    grad_norm_params, grad_qkv_bias, grad_up_bias, grad_out_bias = lax.psum(
        (norm_terms, qkv_full, up_full, out_bias_part), ("dp", "tensor")
    )
    return (
        block_out,
        input_grad,
        grad_w_qkv,
        grad_w_out,
        grad_w_up,
        grad_w_down,
        grad_norm_params,
        grad_qkv_bias,
        grad_up_bias,
        grad_out_bias,
    )


def solution(mesh):
    placed = (
        P("dp", None),
        P(),
        P(),
        P(),
        P(),
        P(None, "tensor"),
        P("tensor"),
        P("tensor", None),
        P(None, "tensor"),
        P("tensor"),
        P("tensor", None),
        P(),
        P("dp", None),
    )
    return jax.shard_map(
        per_device,
        mesh=mesh,
        in_specs=placed,
        out_specs=(
            P("dp", None),
            P("dp", None),
            P("dp", "tensor"),
            P("tensor", "dp"),
            P("dp", "tensor"),
            P("tensor", "dp"),
            P(),
            P(),
            P(),
            P(),
        ),
        check_vma=False,
    )
```

profile of v0, /device:TPU:0, one launch (start us, length us, event | category | flops | bytes accessed | tf_op | source)
XLA Modules:
  0.0 1126.1 jit_solution(10098458001995248072)
XLA Ops:
  8.3 3.0 convert_reduce_fusion
  11.7 1.2 fusion.18
  13.3 2.8 fusion.44
  16.1 8.9 convolution_add_fusion
  25.1 6.6 copy.63
  31.6 4.8 fusion.66
  36.4 2.9 copy.99
  39.3 2.9 slice.165
  42.3 3.0 copy.100
  45.3 2.0 fusion.36
  47.3 3.3 subtract_convert_fusion.1
  53.6 1.2 exponential_reduce_fusion
  54.8 2.2 convolution_convert_fusion.1
  57.0 2.4 convolution_convert_fusion
  59.4 1.6 multiply_reduce_fusion
  61.0 1.1 fusion.27
  62.1 1.4 exponential_reduce_fusion.1
  63.5 2.2 convolution_convert_fusion.2
  65.7 1.6 multiply_reduce_fusion.1
  67.3 1.5 fusion.48
  68.9 1.3 multiply_convert_fusion.2
  71.8 1.7 multiply_convert_fusion.1
  74.2 1.6 add_bitcast_fusion
  78.1 1.4 fusion.33
  79.6 2.7 convert_reduce_fusion.2
  82.2 4.7 copy.83
  87.0 11.9 %fusion.72 = f32[1024,2048]{1,0:T(8,128)} fusion(bf16[1024,1536]{0,1:T(8,128)(2,1)} %bitcast.118, bf16[2048,1536]{1,0:T(8,128)(2,1)} %param.18), kind=kOutput, calls=%fused_computation.135 | convolution fusion | flops 6442450944 | bytes 17825792 | tf_op jit(solution)/shard_map/te,ce->tc/dot_general | solution.py:208
  99.0 11.8 %fusion.59 = f32[1024,2048]{1,0:T(8,128)S(1)} fusion(bf16[2048,2048]{1,0:T(8,128)(2,1)} %param.21, bf16[1024,2048]{1,0:T(8,128)(2,1)S(1)} %copy-done.2, f32[2048]{0:T(1024)S(1)} %copy-done.27, f32[2048]{0:T(1024)S(1)} %copy-done.29, f32[1024]{0:T(1024)S(1)} %add_rsqrt_fusion, f32[1024]{0:T(1024)S(1)} %broadcast_multiply_fusion.2), kind=kOutput, calls=%fused_computation.130 | convolution fusion | flops 8602517504 | bytes 20996096 | tf_op jit(solution)/shard_map/dot_general | solution.py:170
  110.8 29.3 %convert_reduce_fusion.1 = (f32[2048]{0:T(1024)S(1)}, bf16[1024,2048]{1,0:T(8,128)(2,1)}, f32[1024,2048]{1,0:T(8,128)}) fusion(f32[1024,2048]{1,0:T(8,128)S(1)} %fusion.59, f32[2048]{0:T(1024)S(1)} %copy-done.19, bf16[1024,2048]{1,0:T(8,128)(2,1)S(1)} %copy-done.5, bf16[2048,2048]{1,0:T(8,128)(2,1)S(1)} %bitcast.133), kind=kOutput, calls=%fused_computation.26 | convolution fusion | flops 8747218944 | bytes 33570816 | tf_op jit(solution)/shard_map/td,fd->tf/dot_general | solution.py:179
  140.1 8.0 multiply_convert_fusion
  148.1 14.7 %fusion.71 = f32[1024,2048]{1,0:T(8,128)} fusion(bf16[1024,2048]{1,0:T(8,128)(2,1)S(1)} %multiply_convert_fusion, bf16[2048,2048]{1,0:T(8,128)(2,1)} %param.23), kind=kOutput, calls=%fused_computation.134 | convolution fusion | flops 8589934592 | bytes 20971520 | tf_op jit(solution)/shard_map/dot_general | solution.py:172
  162.9 17.1 %multiply_add_fusion = (f32[1024,2048]{1,0:T(8,128)}, f32[1024,2048]{1,0:T(8,128)}) fusion(f32[1024,2048]{1,0:T(8,128)} %fusion.72, f32[2048]{0:T(1024)S(1)} %copy-done.29, f32[2048]{0:T(1024)S(1)} %copy-done.26, bf16[1024,2048]{1,0:T(8,128)(2,1)} %get-tuple-element.27, bf16[2048,2048]{1,0:T(8,128)(2,1)} %param.21), kind=kOutput, calls=%fused_computation.27 | convolution fusion | flops 8596226048 | bytes 37765120 | tf_op jit(solution)/shard_map/tf,cf->tc/dot_general | solution.py:184
  180.0 9.2 convolution_add_fusion.1
  189.3 6.5 fusion.40
  197.5 2.3 convert_reduce_fusion.3
  199.8 554.5 %all-reduce.7.cloned.1.call-done = (f32[1024,2048]{1,0:T(8,128)}, f32[1024,2048]{1,0:T(8,128)}) async-done(((f32[1024,2048]{1,0:T(8,128)}, f32[1024,2048]{1,0:T(8,128)}), (f32[1024,2048]{1,0:T(8,128)}, f32[1024,2048]{1,0:T(8,128)})) %all-reduce.7.cloned.1.call-update) | async-done | bytes 16777232 | tf_op jit(solution)/shard_map/psum | solution.py:177
  754.3 11.8 %fusion.64 = (f32[1024]{0:T(1024)S(1)}, f32[1024]{0:T(1024)S(1)}, f32[2048]{0:T(1024)S(1)}, f32[2048]{0:T(1024)S(1)}, f32[2048]{0:T(1024)S(1)}, /*index=5*/f32[2048]{0:T(1024)S(1)}) fusion(f32[1024,2048]{1,0:T(8,128)} %get-tuple-element.25, f32[1024]{0:T(1024)S(1)} %copy-done.17, f32[1024]{0:T(1024)S(1)} %copy-done.15, bf16[1024,2048]{1,0:T(8,128)(2,1)} %param.13, ...), kind=kLoop, calls=%fused_computation.132 | loop fusion | flops 25155584 | bytes 29409280 | tf_op jit(solution)/shard_map/reduce_sum | solution.py:133
  766.9 14.5 %fusion.61 = f32[2048,1536]{1,0:T(8,128)} fusion(bf16[1024,1536]{0,1:T(8,128)(2,1)} %bitcast.119, bf16[1024,2048]{1,0:T(8,128)(2,1)} %param.13, f32[2048]{0:T(1024)S(1)} %copy-done.24, f32[2048]{0:T(1024)S(1)} %copy-done.26, f32[1024]{0:T(1024)S(1)} %copy-done.17, f32[1024]{0:T(1024)S(1)} %copy-done.15), kind=kOutput, calls=%fused_computation.131 | convolution fusion | flops 6455033856 | bytes 19947520 | tf_op jit(solution)/shard_map/tc,te->ce/dot_general | solution.py:204
  781.5 17.7 %fusion.73 = f32[2048,2048]{1,0:T(8,128)} fusion(bf16[1024,2048]{1,0:T(8,128)(2,1)} %copy-done.8, bf16[1024,2048]{1,0:T(8,128)(2,1)} %param.25), kind=kOutput, calls=%fused_computation.136 | convolution fusion | flops 8589934592 | bytes 25165824 | tf_op jit(solution)/shard_map/tf,td->fd/dot_general | solution.py:182
  799.9 15.9 %fusion.57 = f32[2048,2048]{1,0:T(8,128)} fusion(bf16[1024,2048]{1,0:T(8,128)(2,1)} %get-tuple-element.27, bf16[1024,2048]{1,0:T(8,128)(2,1)} %param.13, f32[2048]{0:T(1024)S(1)} %copy-done.28, f32[2048]{0:T(1024)S(1)} %copy-done.29, f32[1024]{0:T(1024)S(1)} %copy-done.17, f32[1024]{0:T(1024)S(1)} %copy-done.15), kind=kOutput, calls=%fused_computation.129 | convolution fusion | flops 8602517504 | bytes 25190400 | tf_op jit(solution)/shard_map/tc,tf->cf/dot_general | solution.py:183
  816.5 16.0 %fusion.15 = (f32[1024,2048]{1,0:T(8,128)}, bf16[1024,2048]{1,0:T(8,128)(2,1)}) fusion(bf16[1024,2048]{1,0:T(8,128)(2,1)} %param.13, f32[1024,2048]{1,0:T(8,128)} %get-tuple-element.25, bf16[1024,2048]{1,0:T(8,128)(2,1)} %param.25, f32[1024]{0:T(1024)S(1)} %broadcast_multiply_fusion, f32[1024]{0:T(1024)S(1)} %broadcast_multiply_fusion.1, ...), kind=kLoop, calls=%fused_computation.19 | loop fusion | flops 25165824 | bytes 37773312 | tf_op jit(solution)/shard_map/add | solution.py:135
  832.5 73.3 %all-reduce.5.cloned.1.call-done = (f32[4,2048]{1,0:T(4,128)}, f32[6144]{0:T(1024)}, f32[8192]{0:T(1024)}, f32[2048]{0:T(1024)}) async-done(((f32[4,2048]{1,0:T(4,128)}, f32[6144]{0:T(1024)}, f32[8192]{0:T(1024)}, f32[2048]{0:T(1024)}), (f32[4,2048]{1,0:T(4,128)}, f32[6144]{0:T(1024)}, f32[8192]{0:T(1024)}, f32[2048]{0:T(1024)})) %all-reduce.5.cloned.1.call-update) | async-done | bytes 98320 | tf_op jit(solution)/shard_map/psum | solution.py:240
  905.8 86.9 %reduce-scatter.11.cloned.1.call-done = f32[2048,256]{1,0:T(8,128)} async-done(((f32[2048,2048]{1,0:T(8,128)}), f32[2048,256]{1,0:T(8,128)}) %reduce-scatter.11.cloned.1.call-update) | async-done | bytes 2097168 | tf_op jit(solution)/shard_map/reduce_scatter | solution.py:215
  992.7 120.2 %reduce-scatter.9.cloned.1.call-done = f32[256,2048]{1,0:T(8,128)} async-done(((f32[2048,2048]{1,0:T(8,128)}), f32[256,2048]{1,0:T(8,128)}) %reduce-scatter.9.cloned.1.call-update) | async-done | bytes 2097168 | tf_op jit(solution)/shard_map/reduce_scatter | solution.py:214
  1112.9 1.4 copy.119
  1114.3 1.3 copy.120
  1115.6 1.4 copy.121
  1117.0 1.3 copy.122
  (110 shorter events, 12.7 us)
Async XLA Ops:
  8.0 49.0 %copy-start = (bf16[512,2048]{1,0:T(8,128)(2,1)S(1)}, bf16[512,2048]{1,0:T(8,128)(2,1)}, u32[]{:S(2)}) copy-start(bf16[512,2048]{1,0:T(8,128)(2,1)} %param.20) | copy-start | bytes 6291460
  8.0 746.3 %all-reduce.7.cloned.1.call-start = ((), (), s32[]{:S(2)}) async-start(), calls=%async_computation.9 | async-start | bytes 33554432 | tf_op jit(solution)/shard_map/psum | solution.py:177
  8.1 3.6 copy-start.1
  8.3 7.8 copy-start.21
  8.3 7.8 copy-start.22
  8.3 7.8 copy-start.23
  8.3 7.8 copy-start.25
  11.7 87.2 %copy-start.14 = (f32[1024]{0:T(1024)}, f32[1024]{0:T(1024)S(1)}, u32[]{:S(2)}) copy-start(f32[1024]{0:T(1024)S(1)} %broadcast_multiply_fusion.2) | copy-start | bytes 12292
  12.9 86.0 %copy-start.16 = (f32[1024]{0:T(1024)}, f32[1024]{0:T(1024)S(1)}, u32[]{:S(2)}) copy-start(f32[1024]{0:T(1024)S(1)} %add_rsqrt_fusion) | copy-start | bytes 12292
  47.3 4.3 copy-start.9
  51.6 3.2 slice-start
  52.5 2.3 slice-start.1
  54.8 2.2 copy-start.4
  75.8 1.3 copy-start.6
  75.8 1.3 copy-start.7
  86.9 11.9 %copy-start.2 = (bf16[1024,2048]{1,0:T(8,128)(2,1)S(1)}, bf16[1024,2048]{1,0:T(8,128)(2,1)}, u32[]{:S(2)}) copy-start(bf16[1024,2048]{1,0:T(8,128)(2,1)} %param.13) | copy-start | bytes 12582916
  86.9 12.0 %copy-start.27 = (f32[2048]{0:T(1024)S(1)}, f32[2048]{0:T(1024)}, u32[]{:S(2)}) copy-start(f32[2048]{0:T(1024)} %param.17) | copy-start | bytes 24580
  86.9 12.0 %copy-start.29 = (f32[2048]{0:T(1024)S(1)}, f32[2048]{0:T(1024)}, u32[]{:S(2)}) copy-start(f32[2048]{0:T(1024)} %param.16) | copy-start | bytes 24580
  87.0 23.8 %slice-start.2 = ((s8[8388608]{0:T(1024)(128)(4,1)}), s8[4194304]{0:T(1024)(128)(4,1)S(1)}, s32[]{:S(2)}) async-start(s8[8388608]{0:T(1024)(128)(4,1)} %bitcast.132), calls=%async_computation.12 | async-start | bytes 8388608
  98.9 11.9 %copy-start.5 = (bf16[1024,2048]{1,0:T(8,128)(2,1)S(1)}, bf16[1024,2048]{1,0:T(8,128)(2,1)}, u32[]{:S(2)}) copy-start(bf16[1024,2048]{1,0:T(8,128)(2,1)} %param.25) | copy-start | bytes 12582916
  98.9 11.9 %copy-start.19 = (f32[2048]{0:T(1024)S(1)}, f32[2048]{0:T(1024)}, u32[]{:S(2)}) copy-start(f32[2048]{0:T(1024)} %param.22) | copy-start | bytes 24580
  98.9 11.9 %slice-start.3 = ((s8[8388608]{0:T(1024)(128)(4,1)}), s8[4194304]{0:T(1024)(128)(4,1)S(1)}, s32[]{:S(2)}) async-start(s8[8388608]{0:T(1024)(128)(4,1)} %bitcast.132), calls=%async_computation.13 | async-start | bytes 8388608
  110.8 29.3 %copy-start.3 = (f32[1024,2048]{1,0:T(8,128)}, f32[1024,2048]{1,0:T(8,128)S(1)}, u32[]{:S(2)}) copy-start(f32[1024,2048]{1,0:T(8,128)S(1)} %fusion.59) | copy-start | bytes 25165828
  148.1 14.8 %copy-start.8 = (bf16[1024,2048]{1,0:T(8,128)(2,1)}, bf16[1024,2048]{1,0:T(8,128)(2,1)S(1)}, u32[]{:S(2)}) copy-start(bf16[1024,2048]{1,0:T(8,128)(2,1)S(1)} %multiply_convert_fusion) | copy-start | bytes 12582916
  148.1 14.7 %copy-start.26 = (f32[2048]{0:T(1024)S(1)}, f32[2048]{0:T(1024)}, u32[]{:S(2)}) copy-start(f32[2048]{0:T(1024)} %param.14) | copy-start | bytes 24580
  162.9 17.1 %copy-start.10 = (bf16[2,256,512]{2,1,0:T(8,128)(2,1)S(1)}, bf16[2,256,512]{2,1,0:T(8,128)(2,1)}, u32[]{:S(2)}) copy-start(bf16[2,256,512]{2,1,0:T(8,128)(2,1)} %convolution_convert_fusion.1) | copy-start | bytes 1572868
  162.9 17.1 %copy-start.11 = (bf16[2,256,512]{2,1,0:T(8,128)(2,1)S(1)}, bf16[2,256,512]{2,1,0:T(8,128)(2,1)}, u32[]{:S(2)}) copy-start(bf16[2,256,512]{2,1,0:T(8,128)(2,1)} %convolution_convert_fusion.2) | copy-start | bytes 1572868
  189.2 643.2 %reduce-scatter.7.cloned.1.call-start = ((), (), s32[]{:S(2)}) async-start(), calls=%async_computation.5 | async-start | bytes 4718592 | tf_op jit(solution)/shard_map/reduce_scatter | solution.py:213
  195.7 0.7 copy-start.18
  195.7 558.6 %copy-start.15 = (f32[1024]{0:T(1024)S(1)}, f32[1024]{0:T(1024)}, u32[]{:S(2)}) copy-start(f32[1024]{0:T(1024)} %copy-done.14) | copy-start | bytes 12292
  195.7 558.6 %copy-start.17 = (f32[1024]{0:T(1024)S(1)}, f32[1024]{0:T(1024)}, u32[]{:S(2)}) copy-start(f32[1024]{0:T(1024)} %copy-done.16) | copy-start | bytes 12292
  195.8 710.0 %all-reduce.5.cloned.1.call-start = ((), (), s32[]{:S(2)}) async-start(), calls=%async_computation.8 | async-start | bytes 196608 | tf_op jit(solution)/shard_map/psum | solution.py:240
  197.2 569.0 %copy-start.13 = (f32[6144]{0:T(1024)}, f32[6144]{0:T(1024)S(1)}, u32[]{:S(2)}) copy-start(f32[6144]{0:T(1024)S(1)} %dynamic_update_slice.6) | copy-start | bytes 73732
  197.5 568.6 %copy-start.12 = (f32[8192]{0:T(1024)}, f32[8192]{0:T(1024)S(1)}, u32[]{:S(2)}) copy-start(f32[8192]{0:T(1024)S(1)} %dynamic_update_slice.7) | copy-start | bytes 98308
  754.3 12.5 %copy-start.24 = (f32[2048]{0:T(1024)S(1)}, f32[2048]{0:T(1024)}, u32[]{:S(2)}) copy-start(f32[2048]{0:T(1024)} %param.15) | copy-start | bytes 24580
  766.8 138.9 %reduce-scatter.5.cloned.1.call-start = ((), (), s32[]{:S(2)}) async-start(), calls=%async_computation.4 | async-start | bytes 14155776 | tf_op jit(solution)/shard_map/reduce_scatter | solution.py:212
  781.4 211.3 %reduce-scatter.11.cloned.1.call-start = ((), (), s32[]{:S(2)}) async-start(), calls=%async_computation.7 | async-start | bytes 18874368 | tf_op jit(solution)/shard_map/reduce_scatter | solution.py:215
  799.2 0.7 copy-start.28
  799.2 313.7 %reduce-scatter.9.cloned.1.call-start = ((), (), s32[]{:S(2)}) async-start(), calls=%async_computation.6 | async-start | bytes 18874368 | tf_op jit(solution)/shard_map/reduce_scatter | solution.py:214
  815.8 0.7 copy-start.20
Sparse Core Ops, SparseCore 0:
  189.3 564.9 all-reduce.6
  766.9 138.7 all-reduce.4
Sparse Core Ops, SparseCore 1:
  195.8 53.6 reduce-scatter.6
  781.5 91.2 reduce-scatter.4
  876.8 115.9 reduce-scatter.10
  996.9 116.0 reduce-scatter.8
where the time goes:
time: 1130 us
  waiting for transfers between devices  835 us (74%)
  matrix products  176 us (16%)
  other arithmetic  62 us (5%)
  local copies, waits for them, and re-layouts  36.2 us (3%)
  between operations  16.4 us (1%)
    psum x1, waiting for transfers between devices, per_device(): branch_total = lax.psum(branch_terms, 'tensor')  555 us
    reduce_scatter x1, waiting for transfers between devices, per_device(): lax.psum_scatter(grad_up_local, 'dp', scatter_dimension=0, tiled=True)  120 us
    reduce_scatter x1, waiting for transfers between devices, per_device(): lax.psum_scatter(grad_down_local, 'dp', scatter_dimension=1, tiled=True)  86.9 us
    psum x1, waiting for transfers between devices, per_device(): lax.psum((norm_terms, qkv_full, up_full, out_bias_part), ('dp', 'tensor'))  73.3 us
    dot_general x1, matrix products, per_device(): jnp.einsum('td,fd->tf', cotangent, w_down, preferred_element_type=jnp.flo...  29.3 us
  transfers between devices with their start and end apart: 6, of which 4 were waited for; matrix products, arithmetic and copies ran while one was open for 8% of the time, Pallas kernels for 0%

commit v1 on v0

--- a/solution.py
+++ b/solution.py
@@ -2,6 +2,7 @@
 import jax.numpy as jnp
 from jax import lax
 from jax.sharding import PartitionSpec as P
+from jax.lax import all_gather
 
 H = 8
 HD = 256
@@ -174,7 +175,8 @@
     )
     share_rows = row_count // lax.axis_size("tensor")
     row_start = lax.axis_index("tensor") * share_rows
-    branch_total = lax.psum(branch_terms, "tensor")
+    w2 = all_gather(branch_terms, "tensor")
+    branch_total = jnp.sum(w2, axis=0)
     block_out = (tokens_f + branch_total + out_bias).astype(jnp.bfloat16)
     hidden_grad = jnp.einsum("td,fd->tf", cotangent, w_down, preferred_element_type=jnp.float32)
     gelu_pull = jax.vjp(lambda pre_act: jax.nn.gelu(pre_act, approximate=False), up_pre)[1]

time: 1130 us -> 1160 us (1.027)
  other arithmetic: 62 us -> 78.9 us
    all_gather x0 -> x1, waiting for transfers between devices: none -> 498 us  [per_device(): w2 = all_gather(branch_terms, 'tensor')]
    psum x1, waiting for transfers between devices: 555 us -> 246 us  [per_device(): normed_grad = lax.psum(normed_part, 'tensor')]
    reduce_scatter x1, waiting for transfers between devices: 120 us -> 0.01 us  [per_device(): lax.psum_scatter(grad_up_local, 'dp', scatter_dimension=0, tiled=True)]
    reduce_scatter x1, waiting for transfers between devices: 86.9 us -> 0.01 us  [per_device(): lax.psum_scatter(grad_down_local, 'dp', scatter_dimension=1, tiled=True)]
    psum x1, waiting for transfers between devices: 73.3 us -> 98.3 us  [per_device(): lax.psum((norm_terms, qkv_full, up_full, out_bias_part), ('dp', 'tensor'))]
    reduce_sum x0 -> x1, other arithmetic: none -> 16.1 us  [per_device(): branch_total = jnp.sum(w2, axis=0)]
  transfers between devices with their start and end apart: 6 -> 7, of which waited for: 4 -> 3; matrix products, arithmetic and copies ran while one was open for 8% -> 12% of each run, Pallas kernels for 0% -> 0%
where the time goes in v1:
time: 1160 us; the launch traced here: 1150 us
  waiting for transfers between devices  842 us (73%)
  matrix products  179 us (15%)
  other arithmetic  78.9 us (7%)
  local copies, waits for them, and re-layouts  37.5 us (3%)
  between operations  16.3 us (1%)
    all_gather x1, waiting for transfers between devices, per_device(): w2 = all_gather(branch_terms, 'tensor')  498 us
    psum x1, waiting for transfers between devices, per_device(): normed_grad = lax.psum(normed_part, 'tensor')  246 us
    psum x1, waiting for transfers between devices, per_device(): lax.psum((norm_terms, qkv_full, up_full, out_bias_part), ('dp', 'tensor'))  98.3 us
    dot_general x1, matrix products, per_device(): jnp.einsum('td,fd->tf', cotangent, w_down, preferred_element_type=jnp.flo...  29.3 us
  transfers between devices with their start and end apart: 7, of which 3 were waited for; matrix products, arithmetic and copies ran while one was open for 12% of the time, Pallas kernels for 0%

profile of v1, /device:TPU:0, one launch (start us, length us, event | category | flops | bytes accessed | tf_op | source)
XLA Modules:
  0.0 1154.4 jit_solution(6274559366605380828)
XLA Ops:
  8.3 3.1 convert_reduce_fusion
  11.9 1.2 fusion.18
  13.1 2.7 fusion.44
  15.8 11.5 %convolution_add_fusion = f32[1024,1536]{1,0:T(8,128)} fusion(bf16[2048,1536]{1,0:T(8,128)(2,1)} %param.18, f32[1536]{0:T(1024)S(1)} %copy-done.33, bf16[1024,2048]{1,0:T(8,128)(2,1)S(1)} %copy-done.1, f32[2048]{0:T(1024)S(1)} %copy-done.34, f32[2048]{0:T(1024)S(1)} %copy-done.36, f32[1024]{0:T(1024)S(1)} %add_rsqrt_fusion, ...), kind=kOutput, calls=%fused_computation.45 | convolution fusion | flops 6456606720 | bytes 16807936 | tf_op jit(solution)/shard_map/dot_general | solution.py:163
  27.4 6.6 copy.63
  34.0 4.8 fusion.66
  38.8 2.9 copy.99
  41.7 2.9 slice.165
  44.6 3.1 copy.100
  47.7 2.0 fusion.36
  49.7 3.2 subtract_convert_fusion.1
  54.8 1.1 fusion.27
  55.9 1.2 exponential_reduce_fusion.1
  57.4 2.4 convolution_convert_fusion
  60.4 1.6 multiply_reduce_fusion.1
  62.0 1.5 fusion.48
  63.6 1.8 multiply_convert_fusion.2
  68.5 1.2 exponential_reduce_fusion
  69.7 1.6 multiply_reduce_fusion
  71.3 1.4 multiply_convert_fusion.1
  73.5 1.6 add_bitcast_fusion
  77.5 1.3 fusion.33
  78.8 2.6 convert_reduce_fusion.2
  81.4 4.7 copy.83
  86.1 12.0 %fusion.72 = f32[1024,2048]{1,0:T(8,128)} fusion(bf16[1024,1536]{0,1:T(8,128)(2,1)} %bitcast.120, bf16[2048,1536]{1,0:T(8,128)(2,1)} %param.18), kind=kOutput, calls=%fused_computation.135 | convolution fusion | flops 6442450944 | bytes 17825792 | tf_op jit(solution)/shard_map/te,ce->tc/dot_general | solution.py:210
  98.1 11.8 %fusion.59 = f32[1024,2048]{1,0:T(8,128)S(1)} fusion(bf16[2048,2048]{1,0:T(8,128)(2,1)} %param.21, bf16[1024,2048]{1,0:T(8,128)(2,1)S(1)} %copy-done.2, f32[2048]{0:T(1024)S(1)} %copy-done.39, f32[2048]{0:T(1024)S(1)} %copy-done.38, f32[1024]{0:T(1024)S(1)} %add_rsqrt_fusion, f32[1024]{0:T(1024)S(1)} %broadcast_multiply_fusion.2), kind=kOutput, calls=%fused_computation.130 | convolution fusion | flops 8602517504 | bytes 20996096 | tf_op jit(solution)/shard_map/dot_general | solution.py:171
  110.0 29.3 %convert_reduce_fusion.1 = (f32[2048]{0:T(1024)S(1)}, bf16[1024,2048]{1,0:T(8,128)(2,1)}, f32[1024,2048]{1,0:T(8,128)}) fusion(f32[1024,2048]{1,0:T(8,128)S(1)} %fusion.59, f32[2048]{0:T(1024)S(1)} %copy-done.31, bf16[1024,2048]{1,0:T(8,128)(2,1)S(1)} %copy-done.12, bf16[2048,2048]{1,0:T(8,128)(2,1)S(1)} %bitcast.135), kind=kOutput, calls=%fused_computation.26 | convolution fusion | flops 8747218944 | bytes 33570816 | tf_op jit(solution)/shard_map/td,fd->tf/dot_general | solution.py:181
  139.4 17.2 %multiply_add_fusion = (f32[1024,2048]{1,0:T(8,128)}, f32[1024,2048]{1,0:T(8,128)}) fusion(f32[1024,2048]{1,0:T(8,128)} %fusion.72, f32[2048]{0:T(1024)S(1)} %copy-done.38, f32[2048]{0:T(1024)S(1)} %copy-done.37, bf16[1024,2048]{1,0:T(8,128)(2,1)} %get-tuple-element.25, bf16[2048,2048]{1,0:T(8,128)(2,1)} %param.21), kind=kOutput, calls=%fused_computation.27 | convolution fusion | flops 8596226048 | bytes 37765120 | tf_op jit(solution)/shard_map/tf,cf->tc/dot_general | solution.py:186
  157.6 5.1 convolution_convert_fusion.1
  162.7 3.8 convolution_convert_fusion.2
  166.5 8.0 multiply_convert_fusion
  174.5 12.8 %fusion.71 = f32[1024,2048]{1,0:T(8,128)S(1)} fusion(bf16[1024,2048]{1,0:T(8,128)(2,1)S(1)} %multiply_convert_fusion, bf16[2048,2048]{1,0:T(8,128)(2,1)} %param.23), kind=kOutput, calls=%fused_computation.134 | convolution fusion | flops 8589934592 | bytes 20971520 | tf_op jit(solution)/shard_map/dot_general | solution.py:173
  187.3 5.9 convolution_add_fusion.1
  194.4 6.5 fusion.40
  202.3 2.0 convert_reduce_fusion.3
  204.3 246.0 %all-reduce.4.cloned.1.call-done = f32[1024,2048]{1,0:T(8,128)} async-done(((f32[1024,2048]{1,0:T(8,128)}), f32[1024,2048]{1,0:T(8,128)}) %all-reduce.4.cloned.1.call-update) | async-done | bytes 8388624 | tf_op jit(solution)/shard_map/psum | solution.py:228
  450.3 14.1 %fusion.64 = (f32[1024]{0:T(1024)S(1)}, f32[1024]{0:T(1024)S(1)}, f32[2048]{0:T(1024)S(1)}, f32[2048]{0:T(1024)S(1)}, f32[2048]{0:T(1024)S(1)}, /*index=5*/f32[2048]{0:T(1024)S(1)}) fusion(f32[1024,2048]{1,0:T(8,128)} %all-reduce.4.cloned.1.call-done, f32[1024]{0:T(1024)S(1)} %copy-done.29, f32[1024]{0:T(1024)S(1)} %copy-done.23, ...), kind=kLoop, calls=%fused_computation.132 | loop fusion | flops 25155584 | bytes 29409280 | tf_op jit(solution)/shard_map/reduce_sum | solution.py:134
  465.1 15.3 %fusion.61 = f32[2048,1536]{1,0:T(8,128)} fusion(bf16[1024,1536]{0,1:T(8,128)(2,1)} %bitcast.121, bf16[1024,2048]{1,0:T(8,128)(2,1)} %param.13, f32[2048]{0:T(1024)S(1)} %copy-done.35, f32[2048]{0:T(1024)S(1)} %copy-done.37, f32[1024]{0:T(1024)S(1)} %copy-done.29, f32[1024]{0:T(1024)S(1)} %copy-done.23), kind=kOutput, calls=%fused_computation.131 | convolution fusion | flops 6455033856 | bytes 19947520 | tf_op jit(solution)/shard_map/tc,te->ce/dot_general | solution.py:206
  480.5 17.4 %fusion.73 = f32[2048,2048]{1,0:T(8,128)} fusion(bf16[1024,2048]{1,0:T(8,128)(2,1)} %copy-done.14, bf16[1024,2048]{1,0:T(8,128)(2,1)} %param.25), kind=kOutput, calls=%fused_computation.136 | convolution fusion | flops 8589934592 | bytes 25165824 | tf_op jit(solution)/shard_map/tf,td->fd/dot_general | solution.py:184
  498.6 15.9 %fusion.57 = f32[2048,2048]{1,0:T(8,128)} fusion(bf16[1024,2048]{1,0:T(8,128)(2,1)} %get-tuple-element.25, bf16[1024,2048]{1,0:T(8,128)(2,1)} %param.13, f32[2048]{0:T(1024)S(1)} %copy-done.40, f32[2048]{0:T(1024)S(1)} %copy-done.38, f32[1024]{0:T(1024)S(1)} %copy-done.29, f32[1024]{0:T(1024)S(1)} %copy-done.23), kind=kOutput, calls=%fused_computation.129 | convolution fusion | flops 8602517504 | bytes 25190400 | tf_op jit(solution)/shard_map/tc,tf->cf/dot_general | solution.py:185
  514.5 497.7 %all-gather.3.cloned.1.call-done = f32[4096,2048]{1,0:T(8,128)} async-done(((f32[1024,2048]{1,0:T(8,128)}), f32[4096,2048]{1,0:T(8,128)}) %all-gather.3.cloned.1.call-update) | async-done | bytes 33554448 | tf_op jit(solution)/shard_map/all_gather | solution.py:178
  1012.2 16.1 %reduce_sum.150 = f32[1024,2048]{1,0:T(8,128)} reduce(f32[4,1024,2048]{2,1,0:T(8,128)} %bitcast.115, f32[]{:T(128)} %constant.47.clone.1), dimensions={0}, to_apply=%region_6.7 | reduce | flops 6291456 | bytes 41943044 | tf_op jit(solution)/shard_map/reduce_sum | solution.py:179
  1028.4 14.8 %fusion.15 = (f32[1024,2048]{1,0:T(8,128)}, bf16[1024,2048]{1,0:T(8,128)(2,1)}) fusion(bf16[1024,2048]{1,0:T(8,128)(2,1)} %param.13, f32[1024,2048]{1,0:T(8,128)} %all-reduce.4.cloned.1.call-done, bf16[1024,2048]{1,0:T(8,128)(2,1)} %param.25, f32[1024]{0:T(1024)S(1)} %broadcast_multiply_fusion, f32[1024]{0:T(1024)S(1)} %broadcast_multiply_fusion.1, ...), kind=kLoop, calls=%fused_computation.19 | loop fusion | flops 25165824 | bytes 37773312 | tf_op jit(solution)/shard_map/add | solution.py:136
  1043.2 98.3 %all-reduce.6.cloned.1.call-done = (f32[4,2048]{1,0:T(4,128)}, f32[6144]{0:T(1024)}, f32[8192]{0:T(1024)}, f32[2048]{0:T(1024)}) async-done(((f32[4,2048]{1,0:T(4,128)}, f32[6144]{0:T(1024)}, f32[8192]{0:T(1024)}, f32[2048]{0:T(1024)}), (f32[4,2048]{1,0:T(4,128)}, f32[6144]{0:T(1024)}, f32[8192]{0:T(1024)}, f32[2048]{0:T(1024)})) %all-reduce.6.cloned.1.call-update) | async-done | bytes 98320 | tf_op jit(solution)/shard_map/psum | solution.py:242
  1141.5 1.4 copy.118
  1142.9 1.3 copy.119
  1144.2 1.4 copy.120
  1145.6 1.3 copy.121
  (136 shorter events, 14.8 us)
Async XLA Ops:
  8.0 49.1 %copy-start = (bf16[512,2048]{1,0:T(8,128)(2,1)S(1)}, bf16[512,2048]{1,0:T(8,128)(2,1)}, u32[]{:S(2)}) copy-start(bf16[512,2048]{1,0:T(8,128)(2,1)} %param.20) | copy-start | bytes 6291460
  8.0 442.3 %all-reduce.4.cloned.1.call-start = ((), (), s32[]{:S(2)}) async-start(), calls=%async_computation.4 | async-start | bytes 16777216 | tf_op jit(solution)/shard_map/psum | solution.py:228
  8.1 3.8 copy-start.1
  8.3 55.3 %copy-start.7 = (pred[512,1024]{1,0:T(8,128)(4,1)}, pred[512,1024]{1,0:T(8,128)(4,1)S(1)}, u32[]{:S(2)}) copy-start(pred[512,1024]{1,0:T(8,128)(4,1)S(1)} %iota_compare_fusion.2) | copy-start | bytes 1572868
  8.3 7.5 copy-start.33
  8.3 7.5 copy-start.34
  8.3 7.5 copy-start.36
  11.9 86.2 %copy-start.22 = (f32[1024]{0:T(1024)}, f32[1024]{0:T(1024)S(1)}, u32[]{:S(2)}) copy-start(f32[1024]{0:T(1024)S(1)} %broadcast_multiply_fusion.2) | copy-start | bytes 12292
  13.1 85.0 %copy-start.28 = (f32[1024]{0:T(1024)}, f32[1024]{0:T(1024)S(1)}, u32[]{:S(2)}) copy-start(f32[1024]{0:T(1024)S(1)} %add_rsqrt_fusion) | copy-start | bytes 12292
  49.7 4.1 copy-start.15
  54.8 2.5 copy-start.11
  55.9 7.7 copy-start.3
  55.9 4.1 slice-start
  57.4 6.2 copy-start.24
  57.4 3.0 slice-start.1
  67.4 6.1 copy-start.9
  68.5 5.0 copy-start.5
  69.7 3.8 copy-start.26
  75.1 1.3 copy-start.13
  86.1 12.0 %copy-start.2 = (bf16[1024,2048]{1,0:T(8,128)(2,1)S(1)}, bf16[1024,2048]{1,0:T(8,128)(2,1)}, u32[]{:S(2)}) copy-start(bf16[1024,2048]{1,0:T(8,128)(2,1)} %param.13) | copy-start | bytes 12582916
  86.1 12.0 %copy-start.38 = (f32[2048]{0:T(1024)S(1)}, f32[2048]{0:T(1024)}, u32[]{:S(2)}) copy-start(f32[2048]{0:T(1024)} %param.16) | copy-start | bytes 24580
  86.1 12.0 %copy-start.39 = (f32[2048]{0:T(1024)S(1)}, f32[2048]{0:T(1024)}, u32[]{:S(2)}) copy-start(f32[2048]{0:T(1024)} %param.17) | copy-start | bytes 24580
  86.1 23.9 %slice-start.2 = ((s8[8388608]{0:T(1024)(128)(4,1)}), s8[4194304]{0:T(1024)(128)(4,1)S(1)}, s32[]{:S(2)}) async-start(s8[8388608]{0:T(1024)(128)(4,1)} %bitcast.134), calls=%async_computation.13 | async-start | bytes 8388608
  98.1 11.9 %copy-start.12 = (bf16[1024,2048]{1,0:T(8,128)(2,1)S(1)}, bf16[1024,2048]{1,0:T(8,128)(2,1)}, u32[]{:S(2)}) copy-start(bf16[1024,2048]{1,0:T(8,128)(2,1)} %param.25) | copy-start | bytes 12582916
  98.1 11.9 %copy-start.31 = (f32[2048]{0:T(1024)S(1)}, f32[2048]{0:T(1024)}, u32[]{:S(2)}) copy-start(f32[2048]{0:T(1024)} %param.22) | copy-start | bytes 24580
  98.1 11.9 %slice-start.3 = ((s8[8388608]{0:T(1024)(128)(4,1)}), s8[4194304]{0:T(1024)(128)(4,1)S(1)}, s32[]{:S(2)}) async-start(s8[8388608]{0:T(1024)(128)(4,1)} %bitcast.134), calls=%async_computation.14 | async-start | bytes 8388608
  110.0 29.3 %copy-start.6 = (f32[1024,2048]{1,0:T(8,128)}, f32[1024,2048]{1,0:T(8,128)S(1)}, u32[]{:S(2)}) copy-start(f32[1024,2048]{1,0:T(8,128)S(1)} %fusion.59) | copy-start | bytes 25165828
  110.0 29.3 %copy-start.37 = (f32[2048]{0:T(1024)S(1)}, f32[2048]{0:T(1024)}, u32[]{:S(2)}) copy-start(f32[2048]{0:T(1024)} %param.14) | copy-start | bytes 24580
  156.6 6.2 copy-start.8
  156.6 6.2 copy-start.25
  156.6 855.7 %all-gather.3.cloned.1.call-start = ((), (), s32[]{:S(2)}) async-start(), calls=%async_computation.9 | async-start | bytes 41943040 | tf_op jit(solution)/shard_map/all_gather | solution.py:178
  157.6 5.2 copy-start.4
  174.5 12.8 %copy-start.14 = (bf16[1024,2048]{1,0:T(8,128)(2,1)}, bf16[1024,2048]{1,0:T(8,128)(2,1)S(1)}, u32[]{:S(2)}) copy-start(bf16[1024,2048]{1,0:T(8,128)(2,1)S(1)} %multiply_convert_fusion) | copy-start | bytes 12582916
  174.5 12.8 %copy-start.16 = (bf16[2,256,512]{2,1,0:T(8,128)(2,1)S(1)}, bf16[2,256,512]{2,1,0:T(8,128)(2,1)}, u32[]{:S(2)}) copy-start(bf16[2,256,512]{2,1,0:T(8,128)(2,1)} %convolution_convert_fusion.1) | copy-start | bytes 1572868
  174.5 12.8 %copy-start.18 = (bf16[2,256,512]{2,1,0:T(8,128)(2,1)S(1)}, bf16[2,256,512]{2,1,0:T(8,128)(2,1)}, u32[]{:S(2)}) copy-start(bf16[2,256,512]{2,1,0:T(8,128)(2,1)} %convolution_convert_fusion.2) | copy-start | bytes 1572868
  193.2 1.1 copy-start.17
  193.2 1.2 copy-start.19
  193.2 850.0 %reduce-scatter.7.cloned.1.call-start = ((), (), s32[]{:S(2)}) async-start(), calls=%async_computation.6 | async-start | bytes 4718592 | tf_op jit(solution)/shard_map/reduce_scatter | solution.py:215
  200.9 249.4 %copy-start.23 = (f32[1024]{0:T(1024)S(1)}, f32[1024]{0:T(1024)}, u32[]{:S(2)}) copy-start(f32[1024]{0:T(1024)} %copy-done.22) | copy-start | bytes 12292
  200.9 249.4 %copy-start.29 = (f32[1024]{0:T(1024)S(1)}, f32[1024]{0:T(1024)}, u32[]{:S(2)}) copy-start(f32[1024]{0:T(1024)} %copy-done.28) | copy-start | bytes 12292
  201.0 940.5 %all-reduce.6.cloned.1.call-start = ((), (), s32[]{:S(2)}) async-start(), calls=%async_computation.10 | async-start | bytes 196608 | tf_op jit(solution)/shard_map/psum | solution.py:242
  202.0 262.4 %copy-start.21 = (f32[6144]{0:T(1024)}, f32[6144]{0:T(1024)S(1)}, u32[]{:S(2)}) copy-start(f32[6144]{0:T(1024)S(1)} %dynamic_update_slice.6) | copy-start | bytes 73732
  202.3 262.1 %copy-start.20 = (f32[8192]{0:T(1024)}, f32[8192]{0:T(1024)S(1)}, u32[]{:S(2)}) copy-start(f32[8192]{0:T(1024)S(1)} %dynamic_update_slice.7) | copy-start | bytes 98308
  450.3 14.8 %copy-start.35 = (f32[2048]{0:T(1024)S(1)}, f32[2048]{0:T(1024)}, u32[]{:S(2)}) copy-start(f32[2048]{0:T(1024)} %param.15) | copy-start | bytes 24580
  465.0 676.4 %reduce-scatter.5.cloned.1.call-start = ((), (), s32[]{:S(2)}) async-start(), calls=%async_computation.5 | async-start | bytes 14155776 | tf_op jit(solution)/shard_map/reduce_scatter | solution.py:214
  480.4 661.1 %reduce-scatter.11.cloned.1.call-start = ((), (), s32[]{:S(2)}) async-start(), calls=%async_computation.8 | async-start | bytes 18874368 | tf_op jit(solution)/shard_map/reduce_scatter | solution.py:217
  497.9 643.6 %reduce-scatter.9.cloned.1.call-start = ((), (), s32[]{:S(2)}) async-start(), calls=%async_computation.7 | async-start | bytes 18874368 | tf_op jit(solution)/shard_map/reduce_scatter | solution.py:216
  1012.2 16.2 %copy-start.32 = (f32[2048]{0:T(1024)S(1)}, f32[2048]{0:T(1024)}, u32[]{:S(2)}) copy-start(f32[2048]{0:T(1024)} %param.24) | copy-start | bytes 24580
  (4 other events, 3.5 us)
Sparse Core Ops, SparseCore 0:
  156.7 293.5 all-reduce.3
  451.8 560.3 all-gather.2
  1019.4 121.9 all-reduce.5
Sparse Core Ops, SparseCore 1:
  201.0 54.2 reduce-scatter.6
  480.5 90.1 reduce-scatter.4
  574.7 115.8 reduce-scatter.10
  694.7 116.0 reduce-scatter.8
